TPU v7x, 256 devices: a whole 4x4x8 slice. The times are simulated.
256 devices in a mesh: rep: 16 (over z_hi, x), tp: 16 (over z_lo, y, core).
Axes of the slice: x: 4, y: 4, z: 8 (z_hi: 4, z_lo: 2; z = z_hi * 2 + z_lo), core: 2. Of those that a mesh axis runs over, the one named last changes fastest.
Arguments:
- tokens: bfloat16 [512, 4096], P(('rep', 'tp')), may hold values from -6 to 6
- conv_state: bfloat16 [3, 512, 8192], P(None, 'rep', 'tp'), may hold values from -6 to 6
- ssm_state: float32 [512, 16, 8192], P('rep', None, 'tp'), may hold values from -6 to 6
- norm_gains: bfloat16 [2, 4096], P(None, ('rep', 'tp')), may hold values from 0.5 to 1.5
- conv_weight: bfloat16 [4, 8192], P(None, ('rep', 'tp')), may hold values from -3 to 3
- conv_skip: bfloat16 [2, 8192], P(None, ('rep', 'tp')), may hold values from -3 to 3
- step_bias: bfloat16 [8192], P(('rep', 'tp')), may hold values from -5 to -1
- decay_log: bfloat16 [16, 8192], P(None, ('rep', 'tp')), may hold values from 0 to 2.796875
- input_proj: bfloat16 [4096, 2, 8192], P(('rep', 'tp')), may hold values from -0.09375 to 0.09375
- select_proj: bfloat16 [8192, 288], P('tp', 'rep'), may hold values from -0.0625 to 0.0625
- step_proj: bfloat16 [256, 8192], P(('rep', 'tp')), may hold values from -0.375 to 0.375
- output_proj: bfloat16 [8192, 4096], P(None, ('rep', 'tp')), may hold values from -0.0625 to 0.0625
- router: bfloat16 [4096, 16], P(('rep', 'tp')), may hold values from -0.09375 to 0.09375
- expert_proj: bfloat16 [4096, 2, 2, 12288], P(('rep', 'tp')), may hold values from -0.09375 to 0.09375
- expert_ids: int32 [512, 2], P(('rep', 'tp')), may hold values from 0 to 15, as said below
Outputs:
- mamba_out: bfloat16 [512, 4096], P(('rep', 'tp'))
- conv_next: bfloat16 [3, 512, 8192], P(None, 'rep', 'tp')
- ssm_next: float32 [512, 16, 8192], P('rep', None, 'tp')
- expert_hidden: bfloat16 [1024, 12288], P('rep', 'tp')
Inputs may be any that keep to these rules, and one draw needn't show every extreme that they name: `expert_ids`: each row names two different experts. Within each aligned block of 2 rows (the rows of one device) each expert e < 2 is named by at most 2 rows.
All inputs are finite; a program needn't handle non-finite values.
Results may differ from a plain program's by a relative error of at most 0.04.
Values may be sent and summed in bfloat16 or wider, within the bound.
A program may use at most 128 MiB of HBM per device.

v0:
```python
import math
import jax
import jax.numpy as jnp
from jax import lax
from jax.sharding import Mesh
from jax.sharding import PartitionSpec as P

CAPACITY = 2
REP_TP = ("rep_0", "rep_1", "tp")
REP = ("rep_0", "rep_1")
epsilon = 1e-05


def in_one_piece(arrays, axis, dim, along):
    widths = [a.shape[along] for a in arrays]
    both = jnp.concatenate(arrays, axis=along)
    out = lax.all_gather(both, axis, axis=dim, tiled=True)
    return tuple(jnp.split(out, [sum(widths[:k]) for k in range(1, len(widths))], axis=along))


def from_everyone(array, axis):
    devices = lax.axis_size(axis)
    return lax.all_to_all(
        jnp.broadcast_to(array[None], (devices, *array.shape)), axis, 0, 0, tiled=True
    )


def joined_along(blocks, dim):
    dims = list(blocks.shape[1:])
    dims[dim] *= blocks.shape[0]
    return jnp.moveaxis(blocks, 0, dim).reshape(dims)


def gathered_copies(array, axis, dim):
    blocks = from_everyone(array, axis)
    return joined_along(blocks, dim)


def gather_packed(arrays, axis, dims):
    ravelled = jnp.concatenate([a.reshape(-1) for a in arrays])
    lines, at, outs = (lax.all_gather(ravelled, axis), 0, [])
    for a, dim in zip(arrays, dims):
        blocks = lines[:, at : at + a.size].reshape(-1, *a.shape)
        outs.append(joined_along(blocks, dim))
        at += a.size
    return tuple(outs)


def over_copies(array, axis):
    return from_everyone(array, axis).astype(jnp.float32).sum(axis=0)


def split_up(array, dim, devices):
    before, after = (array.shape[:dim], array.shape[dim + 1 :])
    return jnp.moveaxis(array.reshape(*before, devices, -1, *after), dim, 0)


def sent_and_summed(array, axis, dim):
    devices = lax.axis_size(axis)
    blocks = lax.all_to_all(split_up(array, dim, devices), axis, 0, 0, tiled=True)
    return jnp.sum(blocks.astype(jnp.float32), axis=0)


def side_by_side(arrays, axis, dim, along):
    widths = [math.prod(a.shape[along:]) for a in arrays]
    both = jnp.concatenate(
        [a.reshape(*a.shape[:along], w) for a, w in zip(arrays, widths)], axis=along
    )
    out = lax.all_gather(both, axis, axis=dim, tiled=True)
    blocks = jnp.split(out, [sum(widths[:k]) for k in range(1, len(widths))], axis=along)
    return tuple((b.reshape(*out.shape[:along], *a.shape[along:]) for a, b in zip(arrays, blocks)))


def own_block(blocks, axes, order):
    dims = [lax.axis_size(a) for a in axes]
    blocks = blocks.reshape(*dims, *blocks.shape[1:])
    blocks = blocks.transpose(*order, *range(len(axes), blocks.ndim))
    blocks = blocks.reshape(-1, *blocks.shape[len(axes) :])
    for k in order:
        blocks = lax.psum_scatter(blocks, axes[k], scatter_dimension=0, tiled=True)
    return blocks[0]


def scatter_axes(array, axes, order, dim):
    devices = lax.axis_size(axes)
    return own_block(split_up(array, dim, devices), axes, order)


def norm_scale(values, gain):
    mean_square = jnp.mean(values * values, axis=-1, keepdims=True)
    return values * lax.rsqrt(mean_square + epsilon) * gain.astype(jnp.float32)


def shards(
    tokens,
    conv_state,
    ssm_state,
    norm_gains,
    conv_weight,
    conv_skip,
    step_bias,
    decay_log,
    input_proj,
    select_proj,
    step_proj,
    output_proj,
    router,
    expert_proj,
    expert_ids,
):
    tp_count = lax.axis_size("tp")
    tp_index = lax.axis_index("tp")
    norm_gain, conv_taps, skip_rows, shift_full, decay_full, router_full = (
        lax.all_gather(norm_gains, REP_TP, axis=1, tiled=True),
        *in_one_piece((conv_weight, conv_skip), REP_TP, 1, 0),
        lax.all_gather(step_bias, REP_TP, axis=0, tiled=True),
        lax.all_gather(decay_log, REP_TP, axis=1, tiled=True),
        lax.all_gather(router, REP_TP, axis=0, tiled=True),
    )
    inner_dev = ssm_state.shape[2]
    channel_start = tp_index * inner_dev
    conv_taps = lax.dynamic_slice_in_dim(conv_taps, channel_start, inner_dev, 1).astype(jnp.float32)
    skip_rows = lax.dynamic_slice_in_dim(skip_rows, channel_start, inner_dev, 1).astype(jnp.float32)
    shift_dev = lax.dynamic_slice_in_dim(shift_full, channel_start, inner_dev, 0).astype(
        jnp.float32
    )
    decay_dev = lax.dynamic_slice_in_dim(decay_full, channel_start, inner_dev, 1).astype(
        jnp.float32
    )
    model_rows = input_proj.shape[0]
    inner_all = input_proj.shape[2]
    input_blocks, expert_blocks, step_blocks = (
        lax.all_to_all(
            input_proj.reshape(model_rows, 1, 2, inner_all),
            "tp",
            split_axis=3,
            concat_axis=0,
            tiled=True,
        ),
        lax.all_to_all(expert_proj, "tp", split_axis=3, concat_axis=0, tiled=True),
        lax.all_to_all(
            step_proj.reshape(step_proj.shape[0], 1, 1, inner_all),
            "tp",
            split_axis=3,
            concat_axis=0,
            tiled=True,
        ),
    )
    output_blocks = lax.all_to_all(output_proj, "tp", split_axis=0, concat_axis=1, tiled=True)
    residual_in = tokens.astype(jnp.float32)
    normed = norm_scale(residual_in, norm_gain[0]).astype(jnp.bfloat16)
    features = gathered_copies(normed, "tp", 0)
    shard_piece = lax.all_gather(input_blocks, REP, axis=0, tiled=True)
    piece_rows = shard_piece.shape[0]
    projected = jnp.dot(
        features, shard_piece.reshape(piece_rows, 2 * inner_dev), preferred_element_type=jnp.float32
    )
    output_rows, step_rows, select_rows = gather_packed(
        (output_blocks, step_blocks, select_proj), REP, (1, 0, 1)
    )
    step_rows = step_rows.reshape(step_rows.shape[0], inner_dev)
    step_rank = step_rows.shape[0]
    state_count = ssm_state.shape[1]
    conv_input = projected[:, :inner_dev]
    gate_z = projected[:, inner_dev:]
    history = conv_state.astype(jnp.float32)
    conv_mix = (
        jnp.sum(conv_taps[:-1, None, :] * history, axis=0)
        + conv_taps[-1] * conv_input
        + skip_rows[0]
    )
    conv_next = jnp.concatenate([conv_state[1:], conv_input.astype(jnp.bfloat16)[None]], axis=0)
    activated = jax.nn.silu(conv_mix)
    select_part = jnp.dot(
        activated.astype(jnp.bfloat16), select_rows, preferred_element_type=jnp.float32
    )
    selected = over_copies(select_part.astype(jnp.bfloat16), "tp").astype(jnp.float32)
    step_low = selected[:, :step_rank].astype(jnp.bfloat16)
    input_map = selected[:, step_rank : step_rank + state_count]
    output_map = selected[:, step_rank + state_count :]
    step_size = jax.nn.softplus(
        jnp.dot(step_low, step_rows, preferred_element_type=jnp.float32) + shift_dev
    )
    decay_rate = -jnp.exp(decay_dev)
    factor = jnp.exp(step_size[:, None, :] * decay_rate[None])
    ssm_next = factor * ssm_state + (step_size * activated)[:, None, :] * input_map[:, :, None]
    readout = jnp.sum(ssm_next * output_map[:, :, None], axis=1) + skip_rows[1] * activated
    gated_out = (readout * jax.nn.silu(gate_z)).astype(jnp.bfloat16)
    output_part = jnp.dot(gated_out, output_rows, preferred_element_type=jnp.float32)
    mixer_out = sent_and_summed(output_part.astype(jnp.bfloat16), "tp", 0)
    residual = residual_in + mixer_out
    mamba_out = residual.astype(jnp.bfloat16)
    moe_in = norm_scale(residual, norm_gain[1]).astype(jnp.bfloat16)
    logits = jnp.dot(moe_in, router_full, preferred_element_type=jnp.float32)
    expert_total = logits.shape[1]
    choose = (
        expert_ids[:, :, None] == jnp.arange(expert_total, dtype=jnp.int32)[None, None, :]
    ).astype(jnp.float32)
    picked = jnp.sum(choose * logits[:, None, :], axis=2)
    first_gate = jax.nn.sigmoid(picked[:, 0] - picked[:, 1])
    second_gate = jax.nn.sigmoid(picked[:, 1] - picked[:, 0])
    window_count = expert_blocks.shape[1]
    window = jnp.arange(window_count, dtype=jnp.int32)
    names_first = expert_ids[:, 0:1] == window[None, :]
    names_second = expert_ids[:, 1:2] == window[None, :]
    zero = jnp.zeros((), jnp.float32)
    gate_w = jnp.where(names_first, first_gate[:, None], zero) + jnp.where(
        names_second, second_gate[:, None], zero
    )
    routed = (names_first | names_second).astype(jnp.int32)
    position = jnp.cumsum(routed, axis=0) - routed
    slot_of = (position[:, :, None] == jnp.arange(CAPACITY, dtype=jnp.int32)[None, None, :]) & (
        routed[:, :, None] > 0
    )
    slot_x = jnp.einsum(
        "tec,td->ecd", slot_of.astype(jnp.bfloat16), moe_in, preferred_element_type=jnp.float32
    )
    slot_local = window_count * CAPACITY
    slot_x = slot_x.astype(jnp.bfloat16).reshape(slot_local, moe_in.shape[1])
    slot_gate = (
        jnp.einsum("tec,te->ec", slot_of.astype(jnp.float32), gate_w)
        .astype(jnp.bfloat16)
        .reshape(slot_local)
    )
    feature_rows = expert_blocks.shape[0]
    replica_rows, gate_all = side_by_side((slot_x, slot_gate), "tp", 0, 1)
    gathered = lax.all_to_all(replica_rows, REP, split_axis=1, concat_axis=0, tiled=True)
    hidden_dev = expert_blocks.shape[3]
    group_rows = tp_count * slot_local
    picked_rows = gathered
    picked_rows = picked_rows.reshape(
        group_rows * lax.axis_size(REP) // slot_local, window_count, CAPACITY, feature_rows
    )
    product = jnp.einsum(
        "gecd,dexf->gecxf", picked_rows, expert_blocks, preferred_element_type=jnp.float32
    )
    summed = scatter_axes(
        product.reshape(group_rows * lax.axis_size(REP), 2 * hidden_dev).astype(jnp.bfloat16),
        REP,
        (1, 0),
        0,
    ).astype(jnp.float32)
    hidden = (
        gate_all.astype(jnp.float32)[:, None]
        * jax.nn.silu(summed[:, :hidden_dev])
        * summed[:, hidden_dev:]
    )
    expert_hidden = hidden.astype(jnp.bfloat16)
    return (mamba_out, conv_next, ssm_next, expert_hidden)


def solution(mesh):
    split = Mesh(mesh.devices.reshape(4, 4, mesh.shape["tp"]), ("rep_0", "rep_1", "tp"))
    return jax.shard_map(
        shards,
        mesh=split,
        in_specs=(
            P(REP_TP, None),
            P(None, REP, "tp"),
            P(REP, None, "tp"),
            P(None, REP_TP),
            P(None, REP_TP),
            P(None, REP_TP),
            P(REP_TP),
            P(None, REP_TP),
            P(REP_TP, None, None),
            P("tp", REP),
            P(REP_TP, None),
            P(None, REP_TP),
            P(REP_TP, None),
            P(REP_TP, None, None, None),
            P(REP_TP, None),
        ),
        out_specs=(P(REP_TP, None), P(None, REP, "tp"), P(REP, None, "tp"), P(REP, "tp")),
        check_vma=False,
    )
```

profile of v0, /device:TPU:2, one launch (start us, length us, event | category | flops | bytes accessed | tf_op | source)
XLA Modules:
  0.0 1973.0 jit_solution(4106802272947335639)
XLA Ops:
  7.2 8.3 copy.135
  16.0 62.6 %reduce.12 = bf16[8192]{0:T(1024)(128)(2,1)S(1)} reduce(bf16[8192,1,1,1]{3,2,1,0:T(2,128)(2,1)} %bitcast.104, bf16[]{:T(256)} %broadcast.160), dimensions={1,2,3}, to_apply=%bitcast.77.reduce_sub_computation | reduce | bytes 32770
  79.2 5.9 all-to-all-start.3
  86.2 5.0 all-to-all-done.3
  91.2 3.5 all-to-all-start.2
  95.0 8.4 reshape.274
  103.4 62.0 %bitcast_reduce_fusion = bf16[8192]{0:T(1024)(128)(2,1)S(1)} fusion(bf16[8192,1,1,1]{3,2,1,0:T(2,128)(2,1)} %reshape.274), kind=kLoop, calls=%fused_computation.72 | loop fusion | bytes 32768 | tf_op jit(solution)/shard_map/all_to_all | solution.py:141
  165.4 2.0 copy.134
  167.4 1.3 reshape.235
  169.6 6.8 copy.129
  176.3 7.7 bitcast_bitcast_fusion
  184.0 5.8 reshape.275
  189.8 18.9 all_to_all.92
  208.7 4.1 reshape.276
  212.8 10.3 copy.152
  223.2 333.4 %all-gather.2 = bf16[256,16,2]{1,2,0:T(2,128)(2,1)S(1)} all-gather(bf16[1,16,2]{1,2,0:T(2,128)(2,1)S(1)} %bitcast.128), channel_id=1, replica_groups=mesh['rep_0'=4,'rep_1'=4,'tp'=16] {'rep_0','rep_1','tp'}, dimensions={0}, use_global_device_ids=true | all-gather | bytes 16448 | tf_op jit(solution)/shard_map/all_gather | solution.py:114
  558.0 3.5 all-to-all-start
  561.5 342.0 %all-gather.1 = bf16[256,32,6]{1,2,0:T(8,128)(2,1)S(1)} all-gather(bf16[1,32,6]{1,2,0:T(8,128)(2,1)S(1)} %maximum_bitcast_fusion.1), channel_id=1, replica_groups=mesh['rep_0'=4,'rep_1'=4,'tp'=16] {'rep_0','rep_1','tp'}, dimensions={0}, use_global_device_ids=true | all-gather | bytes 98688 | tf_op jit(solution)/shard_map/all_gather | solution.py:17
  904.3 5.1 reshape.251
  909.4 1.0 slice.98
  910.4 5.1 reshape.239
  916.6 11.3 copy.132
  927.9 6.0 fusion.24
  934.9 3.6 all-to-all-start.4
  938.5 344.1 %all-gather.3 = bf16[256,32,16]{1,2,0:T(8,128)(2,1)S(1)} all-gather(bf16[1,32,16]{1,2,0:T(8,128)(2,1)S(1)} %bitcast.126), channel_id=1, replica_groups=mesh['rep_0'=4,'rep_1'=4,'tp'=16] {'rep_0','rep_1','tp'}, dimensions={0}, use_global_device_ids=true | all-gather | bytes 263168 | tf_op jit(solution)/shard_map/all_gather | solution.py:117
  1282.9 1.1 reshape.259
  1284.3 98.4 %all-reduce = bf16[8192]{0:T(1024)(128)(2,1)S(1)} all-reduce(bf16[8192]{0:T(1024)(128)(2,1)S(1)} %dynamic-update-slice), channel_id=1, replica_groups=mesh['rep_0'=4,'rep_1'=4,'tp'=16] {'rep_0','rep_1','tp'}, use_global_device_ids=true, to_apply=%add | all-reduce | flops 8192 | bytes 32768
  1382.9 4.4 slice.105
  1387.5 5.1 copy.157
  1392.6 6.5 copy.139
  1399.5 1.4 multiply_reduce_fusion
  1400.9 3.5 convolution_convert_fusion
  1405.3 5.3 all-to-all-start.5
  1410.8 20.2 %copy.142 = bf16[16,2,2,12288]{0,2,1,3:T(2,128)(2,1)} copy(bf16[16,2,2,12288]{3,2,1,0:T(2,128)(2,1)S(1)} %copy-done.1) | data formatting | bytes 3145728 | tf_op args[13]
  1430.9 17.7 reshape.277
  1448.6 328.0 %all_gather.34 = bf16[4096,16]{1,0:T(8,128)(2,1)S(1)} all-gather(bf16[16,16]{1,0:T(8,128)(2,1)S(1)} %copy-done.10), channel_id=1, replica_groups=mesh['rep_0'=4,'rep_1'=4,'tp'=16] {'rep_0','rep_1','tp'}, dimensions={0}, use_global_device_ids=true | all-gather | bytes 131584 | tf_op jit(solution)/shard_map/all_gather | solution.py:118
  1776.6 3.9 all-to-all-start.7
  1782.5 32.2 %all-gather.4 = bf16[16,4,4097]{2,1,0:T(4,128)(2,1)S(1)} all-gather(bf16[1,4,4097]{2,1,0:T(4,128)(2,1)S(1)} %maximum_bitcast_fusion), channel_id=1, replica_groups=mesh['rep_0'=4,'rep_1'=4,'tp'=16] {'tp'}, dimensions={0}, use_global_device_ids=true | all-gather | bytes 557192 | tf_op jit(solution)/shard_map/all_gather | solution.py:69
  1816.0 25.0 %all-to-all-start.6 = ((bf16[64,16,256]{2,0,1:T(8,128)(2,1)}), bf16[64,16,256]{2,0,1:T(8,128)(2,1)S(1)}, u32[]{:S(2)}, u32[]{:S(2)}) async-start(bf16[64,16,256]{2,0,1:T(8,128)(2,1)} %bitcast.95), calls=%async_computation.6 | async-start | bytes 1048576 | tf_op jit(solution)/shard_map/all_to_all | solution.py:227
  1841.1 12.1 reshape.278
  1853.2 26.5 %copy.143 = bf16[16,2,2,16,768]{4,0,3,2,1:T(8,128)(2,1)S(1)} copy(bf16[16,2,2,16,768]{0,2,1,4,3:T(2,128)(2,1)} %bitcast.98) | data formatting | bytes 3145728 | tf_op jit(solution)/shard_map/all_to_all | solution.py:140
  1880.0 1.0 convert_bitcast_fusion
  1880.9 3.2 copy.145
  1884.2 3.3 convert_element_type.118
  1887.5 3.9 copy.146
  1891.5 39.0 %reduce-scatter.3.cloned.1.call-done = bf16[4,64,1536]{2,1,0:T(8,128)(2,1)} async-done(((bf16[16,64,1536]{2,1,0:T(8,128)(2,1)}), bf16[4,64,1536]{2,1,0:T(8,128)(2,1)}) %reduce-scatter.3.cloned.1.call-update) | async-done | bytes 786448 | tf_op jit(solution)/shard_map/reduce_scatter | solution.py:80
  1932.0 32.7 %reduce-scatter.5.cloned.1.call-done = bf16[1,64,1536]{2,1,0:T(8,128)(2,1)} async-done(((bf16[4,64,1536]{2,1,0:T(8,128)(2,1)}), bf16[1,64,1536]{2,1,0:T(8,128)(2,1)}) %reduce-scatter.5.cloned.1.call-update) | async-done | bytes 196624 | tf_op jit(solution)/shard_map/reduce_scatter | solution.py:80
  1964.6 1.0 bitcast_convert_fusion
  (115 shorter events, 15.7 us)
Async XLA Ops:
  7.2 78.0 %copy-start.6 = (bf16[8192,16]{0,1:T(8,128)(2,1)S(1)}, bf16[8192,16]{0,1:T(8,128)(2,1)}, u32[]{:S(2)}) copy-start(bf16[8192,16]{0,1:T(8,128)(2,1)} %param.26) | copy-start | bytes 786436
  7.2 78.7 %copy-start.7 = (bf16[512,18]{0,1:T(8,128)(2,1)S(1)}, bf16[512,18]{0,1:T(8,128)(2,1)}, u32[]{:S(2)}) copy-start(bf16[512,18]{0,1:T(8,128)(2,1)} %param.24) | copy-start | bytes 55300
  79.2 12.0 all-to-all-start.3
  91.2 74.2 %all-to-all-start.2 = ((bf16[16,512,16]{1,2,0:T(8,128)(2,1)}), bf16[16,512,16]{1,2,0:T(8,128)(2,1)S(1)}, u32[]{:S(2)}, u32[]{:S(2)}) async-start(bf16[16,512,16]{1,2,0:T(8,128)(2,1)} %bitcast.96), calls=%async_computation.2 | async-start | bytes 524288 | tf_op jit(solution)/shard_map/all_to_all | solution.py:149
  94.8 809.6 %all-gather.10.cloned.1.call-start = ((), (), s32[]{:S(2)}) async-start(), calls=%async_computation.13 | async-start | bytes 5048320 | tf_op jit(solution)/shard_map/all_gather | solution.py:41
  103.4 66.2 %copy-start.3 = (bf16[16,2,8192]{2,1,0:T(2,128)(2,1)S(1)}, bf16[16,2,8192]{2,1,0:T(2,128)(2,1)}, u32[]{:S(2)}) copy-start(bf16[16,2,8192]{2,1,0:T(2,128)(2,1)} %param.23) | copy-start | bytes 1572868
  169.5 747.1 %all-gather.8.cloned.1.call-start = ((), (), s32[]{:S(2)}) async-start(), calls=%async_computation.10 | async-start | bytes 8912896 | tf_op jit(solution)/shard_map/all_gather | solution.py:153
  208.7 14.5 copy-start.12
  208.7 348.1 %copy-start.5 = (bf16[2,4096]{1,0:T(2,128)(2,1)S(1)}, bf16[2,4096]{1,0:T(2,128)(2,1)}, u32[]{:S(2)}) copy-start(bf16[2,4096]{1,0:T(2,128)(2,1)} %param.15) | copy-start | bytes 49156
  212.8 348.7 %copy-start.11 = (bf16[4,32]{1,0:T(4,128)(2,1)S(1)}, bf16[4,32]{1,0:T(4,128)(2,1)}, u32[]{:S(2)}) copy-start(bf16[4,32]{1,0:T(4,128)(2,1)} %param.19) | copy-start | bytes 772
  212.8 348.7 %copy-start.13 = (bf16[2,32]{1,0:T(2,128)(2,1)S(1)}, bf16[2,32]{1,0:T(2,128)(2,1)}, u32[]{:S(2)}) copy-start(bf16[2,32]{1,0:T(2,128)(2,1)} %param.20) | copy-start | bytes 388
  212.8 691.3 %copy-start.4 = (bf16[3,32,512]{2,1,0:T(8,128)(2,1)S(1)}, bf16[3,32,512]{2,1,0:T(8,128)(2,1)}, u32[]{:S(2)}) copy-start(bf16[3,32,512]{2,1,0:T(8,128)(2,1)} %param.16) | copy-start | bytes 294916
  558.0 346.2 %all-to-all-start = ((bf16[16,2,4096]{2,1,0:T(2,128)(2,1)}), bf16[16,2,4096]{2,1,0:T(2,128)(2,1)S(1)}, u32[]{:S(2)}, u32[]{:S(2)}) async-start(bf16[16,2,4096]{2,1,0:T(2,128)(2,1)} %broadcast_in_dim.24), calls=%async_computation | async-start | bytes 524288 | tf_op jit(solution)/shard_map/all_to_all | solution.py:23
  927.9 10.6 copy-start.9
  933.9 350.1 %copy-start.14 = (bf16[32]{0:T(256)(128)(2,1)S(1)}, bf16[32]{0:T(256)(128)(2,1)}, u32[]{:S(2)}) copy-start(bf16[32]{0:T(256)(128)(2,1)} %param.21) | copy-start | bytes 196
  933.9 448.8 %copy-start.8 = (s32[2,2]{1,0:T(2,128)S(1)}, s32[2,2]{1,0:T(2,128)}, u32[]{:S(2)}) copy-start(s32[2,2]{1,0:T(2,128)} %param.29) | copy-start | bytes 52
  934.9 464.2 %all-to-all-start.4 = ((bf16[16,32,288]{2,1,0:T(8,128)(2,1)}), bf16[16,32,288]{2,1,0:T(8,128)(2,1)S(1)}, u32[]{:S(2)}, u32[]{:S(2)}) async-start(bf16[16,32,288]{2,1,0:T(8,128)(2,1)} %broadcast_in_dim.25), calls=%async_computation.4 | async-start | bytes 786432 | tf_op jit(solution)/shard_map/all_to_all | solution.py:23
  1382.9 4.5 slice-start
  1392.6 6.9 copy-start.2
  1399.3 11.5 copy-start.1
  1405.3 371.3 %all-to-all-start.5 = ((bf16[16,2,4096]{2,1,0:T(2,128)(2,1)}), bf16[16,2,4096]{2,1,0:T(2,128)(2,1)S(1)}, u32[]{:S(2)}, u32[]{:S(2)}) async-start(bf16[16,2,4096]{2,1,0:T(2,128)(2,1)} %reshape.243), calls=%async_computation.5 | async-start | bytes 524288 | tf_op jit(solution)/shard_map/all_to_all | solution.py:60
  1430.9 17.7 copy-start.10
  1776.6 39.4 %all-to-all-start.7 = ((bf16[16,2,24576]{2,1,0:T(2,128)(2,1)}), bf16[16,2,24576]{2,1,0:T(2,128)(2,1)S(1)}, u32[]{:S(2)}, u32[]{:S(2)}) async-start(bf16[16,2,24576]{2,1,0:T(2,128)(2,1)} %reshape.277), calls=%async_computation.7 | async-start | bytes 3145728 | tf_op jit(solution)/shard_map/all_to_all | solution.py:140
  1815.0 38.2 %copy-start = (bf16[64,4097]{1,0:T(8,128)(2,1)}, bf16[64,4097]{1,0:T(8,128)(2,1)S(1)}, u32[]{:S(2)}) copy-start(bf16[64,4097]{1,0:T(8,128)(2,1)S(1)} %reshape.261) | copy-start | bytes 1573252
  1816.0 63.7 %all-to-all-start.6 = ((bf16[64,16,256]{2,0,1:T(8,128)(2,1)}), bf16[64,16,256]{2,0,1:T(8,128)(2,1)S(1)}, u32[]{:S(2)}, u32[]{:S(2)}) async-start(bf16[64,16,256]{2,0,1:T(8,128)(2,1)} %bitcast.95), calls=%async_computation.6 | async-start | bytes 1048576 | tf_op jit(solution)/shard_map/all_to_all | solution.py:227
  1841.0 89.4 %reduce-scatter.3.cloned.1.call-start = ((), (), s32[]{:S(2)}) async-start(), calls=%async_computation.11 | async-start | bytes 3932160 | tf_op jit(solution)/shard_map/reduce_scatter | solution.py:80
  1887.5 43.0 %slice-start.1 = ((bf16[3,32,512]{2,1,0:T(8,128)(2,1)}), bf16[2,32,512]{2,1,0:T(8,128)(2,1)S(1)}, s32[]{:S(2)}) async-start(bf16[3,32,512]{2,1,0:T(8,128)(2,1)} %param.16), calls=%async_computation.15 | async-start | bytes 131072 | tf_op jit(solution)/shard_map/slice | solution.py:172
  1891.4 73.2 %reduce-scatter.5.cloned.1.call-start = ((), (), s32[]{:S(2)}) async-start(), calls=%async_computation.12 | async-start | bytes 983040 | tf_op jit(solution)/shard_map/reduce_scatter | solution.py:80
Sparse Core Ops, SparseCore 0:
  169.6 81.2 all-gather.9
  253.9 117.8 all-gather.7
  1891.5 38.8 reduce-scatter.2
  1932.9 31.7 reduce-scatter.4
where the time goes:
time: 1980 us; the launch traced here: 1970 us
  blocking collectives  1500 us (76%)
  local copies, waits for them, and re-layouts  252 us (13%)
  waiting for transfers between devices  76.8 us (4%)
  other arithmetic  70.1 us (4%)
  starting transfers between devices  51.1 us (3%)
    all_gather x1, blocking collectives, shards(): lax.all_gather(decay_log, REP_TP, axis=1, tiled=True)  344 us
    all_gather x1, blocking collectives, in_one_piece(): out = lax.all_gather(both, axis, axis=dim, tiled=True)  342 us
    all_gather x1, blocking collectives, shards(): lax.all_gather(norm_gains, REP_TP, axis=1, tiled=True)  333 us
    all_gather x1, blocking collectives, shards(): lax.all_gather(router, REP_TP, axis=0, tiled=True)  328 us
    unnamed x1, blocking collectives  98.4 us
    unnamed x48, local copies, waits for them, and re-layouts  91.4 us
    reduce_scatter x2, waiting for transfers between devices, own_block(): blocks = lax.psum_scatter(blocks, axes[k], scatter_dimension=0, tiled=True)  71.6 us
    unnamed x3, other arithmetic  62.6 us
  transfers between devices with their start and end apart: 11, of which 3 were waited for; matrix products, arithmetic and copies ran while one was open for 11% of the time, Pallas kernels for 0%

commit v1 on v0

--- a/solution.py
+++ b/solution.py
@@ -9,6 +9,11 @@
 REP_TP = ("rep_0", "rep_1", "tp")
 REP = ("rep_0", "rep_1")
 epsilon = 1e-05
+
+
+def all_by_exchange(shard, axis, dim):
+    repeated = jnp.stack([shard] * lax.axis_size(axis))
+    return jnp.concatenate(lax.all_to_all(repeated, axis, 0, 0), axis=dim)
 
 
 def in_one_piece(arrays, axis, dim, along):
@@ -114,7 +119,7 @@
         lax.all_gather(norm_gains, REP_TP, axis=1, tiled=True),
         *in_one_piece((conv_weight, conv_skip), REP_TP, 1, 0),
         lax.all_gather(step_bias, REP_TP, axis=0, tiled=True),
-        lax.all_gather(decay_log, REP_TP, axis=1, tiled=True),
+        all_by_exchange(decay_log, REP_TP, 1),
         lax.all_gather(router, REP_TP, axis=0, tiled=True),
     )
     inner_dev = ssm_state.shape[2]

time: 1980 us -> 1650 us (0.83)
  blocking collectives: 1500 us -> 1130 us
  starting transfers between devices: 51.1 us -> 79.7 us
    all_gather x1 -> x0, blocking collectives: 344 us -> none  [shards(): lax.all_gather(decay_log, REP_TP, axis=1, tiled=True)]
    all_to_all x0 -> x1, starting transfers between devices: none -> 27.8 us  [all_by_exchange(): return jnp.concatenate(lax.all_to_all(repeated, axis, 0, 0), axis=dim)]
    unnamed x1, blocking collectives: 98.4 us -> 77.6 us
    unnamed x48 -> x47, local copies, waits for them, and re-layouts: 91.4 us -> 92.1 us
  transfers between devices with their start and end apart: 11 -> 12, of which waited for: 3 -> 3; matrix products, arithmetic and copies ran while one was open for 11% -> 15% of each run, Pallas kernels for 0% -> 0%
where the time goes in v1:
time: 1650 us; the launch traced here: 1640 us
  blocking collectives  1130 us (68%)
  local copies, waits for them, and re-layouts  255 us (15%)
  starting transfers between devices  79.7 us (5%)
  waiting for transfers between devices  76.7 us (5%)
  other arithmetic  71.4 us (4%)
    all_gather x1, blocking collectives, in_one_piece(): out = lax.all_gather(both, axis, axis=dim, tiled=True)  342 us
    all_gather x1, blocking collectives, shards(): lax.all_gather(norm_gains, REP_TP, axis=1, tiled=True)  334 us
    all_gather x1, blocking collectives, shards(): lax.all_gather(router, REP_TP, axis=0, tiled=True)  327 us
    unnamed x47, local copies, waits for them, and re-layouts  92.1 us
    unnamed x1, blocking collectives  77.6 us
    reduce_scatter x2, waiting for transfers between devices, own_block(): blocks = lax.psum_scatter(blocks, axes[k], scatter_dimension=0, tiled=True)  71.6 us
    unnamed x3, other arithmetic  62.6 us
    all_to_all x1, local copies, waits for them, and re-layouts, shards(): lax.all_to_all(step_proj.reshape(step_proj.shape[0], 1, 1, inner_all), 't...  62 us
  transfers between devices with their start and end apart: 12, of which 3 were waited for; matrix products, arithmetic and copies ran while one was open for 15% of the time, Pallas kernels for 0%

profile of v1, /device:TPU:2, one launch (start us, length us, event | category | flops | bytes accessed | tf_op | source)
XLA Modules:
  0.0 1640.1 jit_solution(10133290462967937709)
XLA Ops:
  7.2 8.3 copy.133
  16.0 62.6 %reduce.12 = bf16[8192]{0:T(1024)(128)(2,1)S(1)} reduce(bf16[8192,1,1,1]{3,2,1,0:T(2,128)(2,1)} %bitcast.98, bf16[]{:T(256)} %broadcast.162), dimensions={1,2,3}, to_apply=%bitcast.71.reduce_sub_computation | reduce | bytes 32770
  79.2 5.9 all-to-all-start.3
  86.3 5.0 all-to-all-done.3
  91.3 3.5 all-to-all-start.2
  95.0 8.4 reshape.282
  103.4 62.0 %bitcast_reduce_fusion = bf16[8192]{0:T(1024)(128)(2,1)S(1)} fusion(bf16[8192,1,1,1]{3,2,1,0:T(2,128)(2,1)} %reshape.282), kind=kLoop, calls=%fused_computation.72 | loop fusion | bytes 32768 | tf_op jit(solution)/shard_map/all_to_all | solution.py:146
  165.4 2.0 copy.132
  167.4 1.3 reshape.243
  169.6 6.7 copy.127
  176.3 7.7 bitcast_bitcast_fusion
  184.0 5.8 reshape.283
  189.8 18.9 %all_to_all.97 = bf16[16,2,8192]{2,1,0:T(2,128)(2,1)S(1)} all-to-all(bf16[16,2,8192]{2,1,0:T(2,128)(2,1)S(1)} %reshape.283), channel_id=1, replica_groups=mesh['rep_0'=4,'rep_1'=4,'tp'=16] {'tp'}, dimensions={0} | all-to-all | bytes 1048576 | tf_op jit(solution)/shard_map/all_to_all | solution.py:138
  208.7 4.1 reshape.284
  212.8 10.3 copy.150
  223.2 333.8 %all-gather.2 = bf16[256,16,2]{1,2,0:T(2,128)(2,1)S(1)} all-gather(bf16[1,16,2]{1,2,0:T(2,128)(2,1)S(1)} %bitcast.122), channel_id=1, replica_groups=mesh['rep_0'=4,'rep_1'=4,'tp'=16] {'rep_0','rep_1','tp'}, dimensions={0}, use_global_device_ids=true | all-gather | bytes 16448 | tf_op jit(solution)/shard_map/all_gather | solution.py:119
  558.4 3.5 all-to-all-start
  561.9 342.0 %all-gather.1 = bf16[256,32,6]{1,2,0:T(8,128)(2,1)S(1)} all-gather(bf16[1,32,6]{1,2,0:T(8,128)(2,1)S(1)} %maximum_bitcast_fusion.1), channel_id=1, replica_groups=mesh['rep_0'=4,'rep_1'=4,'tp'=16] {'rep_0','rep_1','tp'}, dimensions={0}, use_global_device_ids=true | all-gather | bytes 98688 | tf_op jit(solution)/shard_map/all_gather | solution.py:22
  904.7 1.4 reshape.285
  906.1 27.8 %all-to-all-start.5 = ((bf16[256,2,256]{2,1,0:T(2,128)(2,1)}), bf16[256,2,256]{2,1,0:T(2,128)(2,1)S(1)}, u32[]{:S(2)}, u32[]{:S(2)}) async-start(bf16[256,2,256]{2,1,0:T(2,128)(2,1)} %reshape.285), calls=%async_computation.5 | async-start | bytes 524288 | tf_op jit(solution)/shard_map/all_to_all | solution.py:16
  934.1 5.1 reshape.261
  939.2 1.0 slice.98
  940.2 5.1 reshape.247
  946.3 12.0 copy.130
  958.3 6.0 fusion.24
  965.4 5.5 all-to-all-start.4
  971.2 77.6 %all-reduce = bf16[8192]{0:T(1024)(128)(2,1)S(1)} all-reduce(bf16[8192]{0:T(1024)(128)(2,1)S(1)} %dynamic-update-slice), channel_id=1, replica_groups=mesh['rep_0'=4,'rep_1'=4,'tp'=16] {'rep_0','rep_1','tp'}, use_global_device_ids=true, to_apply=%add | all-reduce | flops 8192 | bytes 32768
  1049.8 1.1 reshape.250
  1051.0 4.4 slice.105
  1055.6 5.1 copy.155
  1060.6 6.4 copy.137
  1067.4 2.8 multiply_reduce_fusion
  1070.1 3.5 convolution_convert_fusion
  1074.5 4.2 all-to-all-start.6
  1079.0 20.2 %copy.140 = bf16[16,2,2,12288]{0,2,1,3:T(2,128)(2,1)} copy(bf16[16,2,2,12288]{3,2,1,0:T(2,128)(2,1)S(1)} %copy-done.1) | data formatting | bytes 3145728 | tf_op args[13]
  1099.2 17.7 %reshape.287 = bf16[16,2,24576]{2,1,0:T(2,128)(2,1)} reshape(bf16[12288,2,2,16]{3,2,1,0:T(2,128)(2,1)} %bitcast.93) | data formatting | bytes 3145728
  1116.8 327.1 %all_gather.30 = bf16[4096,16]{1,0:T(8,128)(2,1)S(1)} all-gather(bf16[16,16]{1,0:T(8,128)(2,1)S(1)} %copy-done.9), channel_id=1, replica_groups=mesh['rep_0'=4,'rep_1'=4,'tp'=16] {'rep_0','rep_1','tp'}, dimensions={0}, use_global_device_ids=true | all-gather | bytes 131584 | tf_op jit(solution)/shard_map/all_gather | solution.py:123
  1443.9 3.7 all-to-all-start.8
  1449.7 32.2 %all-gather.3 = bf16[16,4,4097]{2,1,0:T(4,128)(2,1)S(1)} all-gather(bf16[1,4,4097]{2,1,0:T(4,128)(2,1)S(1)} %maximum_bitcast_fusion), channel_id=1, replica_groups=mesh['rep_0'=4,'rep_1'=4,'tp'=16] {'tp'}, dimensions={0}, use_global_device_ids=true | all-gather | bytes 557192 | tf_op jit(solution)/shard_map/all_gather | solution.py:74
  1483.2 25.0 %all-to-all-start.7 = ((bf16[64,16,256]{2,0,1:T(8,128)(2,1)}), bf16[64,16,256]{2,0,1:T(8,128)(2,1)S(1)}, u32[]{:S(2)}, u32[]{:S(2)}) async-start(bf16[64,16,256]{2,0,1:T(8,128)(2,1)} %bitcast.89), calls=%async_computation.7 | async-start | bytes 1048576 | tf_op jit(solution)/shard_map/all_to_all | solution.py:232
  1508.3 12.1 reshape.288
  1520.4 26.5 %copy.141 = bf16[16,2,2,16,768]{4,0,3,2,1:T(8,128)(2,1)S(1)} copy(bf16[16,2,2,16,768]{0,2,1,4,3:T(2,128)(2,1)} %bitcast.92) | data formatting | bytes 3145728 | tf_op jit(solution)/shard_map/all_to_all | solution.py:145
  1547.1 1.0 convert_bitcast_fusion
  1548.1 3.2 copy.143
  1551.3 3.3 convert_element_type.118
  1554.7 3.9 copy.144
  1558.6 38.9 %reduce-scatter.3.cloned.1.call-done = bf16[4,64,1536]{2,1,0:T(8,128)(2,1)} async-done(((bf16[16,64,1536]{2,1,0:T(8,128)(2,1)}), bf16[4,64,1536]{2,1,0:T(8,128)(2,1)}) %reduce-scatter.3.cloned.1.call-update) | async-done | bytes 786448 | tf_op jit(solution)/shard_map/reduce_scatter | solution.py:85
  1599.1 32.6 %reduce-scatter.5.cloned.1.call-done = bf16[1,64,1536]{2,1,0:T(8,128)(2,1)} async-done(((bf16[4,64,1536]{2,1,0:T(8,128)(2,1)}), bf16[1,64,1536]{2,1,0:T(8,128)(2,1)}) %reduce-scatter.5.cloned.1.call-update) | async-done | bytes 196624 | tf_op jit(solution)/shard_map/reduce_scatter | solution.py:85
  (117 shorter events, 17.3 us)
Async XLA Ops:
  7.2 78.0 %copy-start.5 = (bf16[8192,16]{0,1:T(8,128)(2,1)S(1)}, bf16[8192,16]{0,1:T(8,128)(2,1)}, u32[]{:S(2)}) copy-start(bf16[8192,16]{0,1:T(8,128)(2,1)} %param.26) | copy-start | bytes 786436
  7.2 78.7 %copy-start.6 = (bf16[512,18]{0,1:T(8,128)(2,1)S(1)}, bf16[512,18]{0,1:T(8,128)(2,1)}, u32[]{:S(2)}) copy-start(bf16[512,18]{0,1:T(8,128)(2,1)} %param.24) | copy-start | bytes 55300
  79.2 12.0 all-to-all-start.3
  91.3 74.2 %all-to-all-start.2 = ((bf16[16,512,16]{1,2,0:T(8,128)(2,1)}), bf16[16,512,16]{1,2,0:T(8,128)(2,1)S(1)}, u32[]{:S(2)}, u32[]{:S(2)}) async-start(bf16[16,512,16]{1,2,0:T(8,128)(2,1)} %bitcast.90), calls=%async_computation.2 | async-start | bytes 524288 | tf_op jit(solution)/shard_map/all_to_all | solution.py:154
  94.8 839.3 %all-gather.9.cloned.1.call-start = ((), (), s32[]{:S(2)}) async-start(), calls=%async_computation.14 | async-start | bytes 5048320 | tf_op jit(solution)/shard_map/all_gather | solution.py:46
  103.4 66.2 %copy-start.2 = (bf16[16,2,8192]{2,1,0:T(2,128)(2,1)S(1)}, bf16[16,2,8192]{2,1,0:T(2,128)(2,1)}, u32[]{:S(2)}) copy-start(bf16[16,2,8192]{2,1,0:T(2,128)(2,1)} %param.23) | copy-start | bytes 1572868
  169.5 776.8 %all-gather.7.cloned.1.call-start = ((), (), s32[]{:S(2)}) async-start(), calls=%async_computation.11 | async-start | bytes 8912896 | tf_op jit(solution)/shard_map/all_gather | solution.py:158
  208.7 14.5 copy-start.11
  208.7 348.5 %copy-start.4 = (bf16[2,4096]{1,0:T(2,128)(2,1)S(1)}, bf16[2,4096]{1,0:T(2,128)(2,1)}, u32[]{:S(2)}) copy-start(bf16[2,4096]{1,0:T(2,128)(2,1)} %param.15) | copy-start | bytes 49156
  212.8 349.1 %copy-start.10 = (bf16[4,32]{1,0:T(4,128)(2,1)S(1)}, bf16[4,32]{1,0:T(4,128)(2,1)}, u32[]{:S(2)}) copy-start(bf16[4,32]{1,0:T(4,128)(2,1)} %param.19) | copy-start | bytes 772
  212.8 349.1 %copy-start.12 = (bf16[2,32]{1,0:T(2,128)(2,1)S(1)}, bf16[2,32]{1,0:T(2,128)(2,1)}, u32[]{:S(2)}) copy-start(bf16[2,32]{1,0:T(2,128)(2,1)} %param.20) | copy-start | bytes 388
  212.8 691.7 %copy-start.8 = (bf16[16,32]{1,0:T(8,128)(2,1)S(1)}, bf16[16,32]{1,0:T(8,128)(2,1)}, u32[]{:S(2)}) copy-start(bf16[16,32]{1,0:T(8,128)(2,1)} %param.22) | copy-start | bytes 3076
  223.1 683.0 %copy-start.3 = (bf16[3,32,512]{2,1,0:T(8,128)(2,1)S(1)}, bf16[3,32,512]{2,1,0:T(8,128)(2,1)}, u32[]{:S(2)}) copy-start(bf16[3,32,512]{2,1,0:T(8,128)(2,1)} %param.16) | copy-start | bytes 294916
  558.4 347.7 %all-to-all-start = ((bf16[16,2,4096]{2,1,0:T(2,128)(2,1)}), bf16[16,2,4096]{2,1,0:T(2,128)(2,1)S(1)}, u32[]{:S(2)}, u32[]{:S(2)}) async-start(bf16[16,2,4096]{2,1,0:T(2,128)(2,1)} %broadcast_in_dim.24), calls=%async_computation | async-start | bytes 524288 | tf_op jit(solution)/shard_map/all_to_all | solution.py:28
  906.1 58.5 %all-to-all-start.5 = ((bf16[256,2,256]{2,1,0:T(2,128)(2,1)}), bf16[256,2,256]{2,1,0:T(2,128)(2,1)S(1)}, u32[]{:S(2)}, u32[]{:S(2)}) async-start(bf16[256,2,256]{2,1,0:T(2,128)(2,1)} %reshape.285), calls=%async_computation.5 | async-start | bytes 524288 | tf_op jit(solution)/shard_map/all_to_all | solution.py:16
  958.3 12.6 copy-start.13
  958.3 90.5 %copy-start.7 = (s32[2,2]{1,0:T(2,128)S(1)}, s32[2,2]{1,0:T(2,128)}, u32[]{:S(2)}) copy-start(s32[2,2]{1,0:T(2,128)} %param.29) | copy-start | bytes 52
  965.4 101.7 %all-to-all-start.4 = ((bf16[16,32,288]{2,1,0:T(8,128)(2,1)}), bf16[16,32,288]{2,1,0:T(8,128)(2,1)S(1)}, u32[]{:S(2)}, u32[]{:S(2)}) async-start(bf16[16,32,288]{2,1,0:T(8,128)(2,1)} %broadcast_in_dim.25), calls=%async_computation.4 | async-start | bytes 786432 | tf_op jit(solution)/shard_map/all_to_all | solution.py:28
  1051.0 4.4 slice-start
  1067.2 11.8 copy-start.1
  1074.5 369.4 %all-to-all-start.6 = ((bf16[16,2,4096]{2,1,0:T(2,128)(2,1)}), bf16[16,2,4096]{2,1,0:T(2,128)(2,1)S(1)}, u32[]{:S(2)}, u32[]{:S(2)}) async-start(bf16[16,2,4096]{2,1,0:T(2,128)(2,1)} %reshape.253), calls=%async_computation.6 | async-start | bytes 524288 | tf_op jit(solution)/shard_map/all_to_all | solution.py:65
  1099.2 17.7 %copy-start.9 = (bf16[16,16]{1,0:T(8,128)(2,1)S(1)}, bf16[16,16]{1,0:T(8,128)(2,1)}, u32[]{:S(2)}) copy-start(bf16[16,16]{1,0:T(8,128)(2,1)} %param.27) | copy-start | bytes 1540
  1443.9 39.3 %all-to-all-start.8 = ((bf16[16,2,24576]{2,1,0:T(2,128)(2,1)}), bf16[16,2,24576]{2,1,0:T(2,128)(2,1)S(1)}, u32[]{:S(2)}, u32[]{:S(2)}) async-start(bf16[16,2,24576]{2,1,0:T(2,128)(2,1)} %reshape.287), calls=%async_computation.8 | async-start | bytes 3145728 | tf_op jit(solution)/shard_map/all_to_all | solution.py:145
  1482.2 38.2 %copy-start = (bf16[64,4097]{1,0:T(8,128)(2,1)}, bf16[64,4097]{1,0:T(8,128)(2,1)S(1)}, u32[]{:S(2)}) copy-start(bf16[64,4097]{1,0:T(8,128)(2,1)S(1)} %reshape.269) | copy-start | bytes 1573252
  1483.2 63.7 %all-to-all-start.7 = ((bf16[64,16,256]{2,0,1:T(8,128)(2,1)}), bf16[64,16,256]{2,0,1:T(8,128)(2,1)S(1)}, u32[]{:S(2)}, u32[]{:S(2)}) async-start(bf16[64,16,256]{2,0,1:T(8,128)(2,1)} %bitcast.89), calls=%async_computation.7 | async-start | bytes 1048576 | tf_op jit(solution)/shard_map/all_to_all | solution.py:232
  1508.2 89.3 %reduce-scatter.3.cloned.1.call-start = ((), (), s32[]{:S(2)}) async-start(), calls=%async_computation.12 | async-start | bytes 3932160 | tf_op jit(solution)/shard_map/reduce_scatter | solution.py:85
  1554.7 42.9 %slice-start.1 = ((bf16[3,32,512]{2,1,0:T(8,128)(2,1)}), bf16[2,32,512]{2,1,0:T(8,128)(2,1)S(1)}, s32[]{:S(2)}) async-start(bf16[3,32,512]{2,1,0:T(8,128)(2,1)} %param.16), calls=%async_computation.16 | async-start | bytes 131072 | tf_op jit(solution)/shard_map/slice | solution.py:177
  1558.5 73.2 %reduce-scatter.5.cloned.1.call-start = ((), (), s32[]{:S(2)}) async-start(), calls=%async_computation.13 | async-start | bytes 983040 | tf_op jit(solution)/shard_map/reduce_scatter | solution.py:85
Sparse Core Ops, SparseCore 0:
  169.6 81.2 all-gather.8
  253.9 111.8 all-gather.6
  1558.7 38.8 reduce-scatter.2
  1599.9 31.7 reduce-scatter.4
